TPU v7x, 32 devices: a whole 2x2x4 slice. The times are simulated.
32 devices in a mesh: curve: 8 (over z, x), level: 4 (over y, core).
Axes of the slice: x: 2, y: 2, z: 4, core: 2. Of those that a mesh axis runs over, the one named last changes fastest.
Arguments:
- right_side: float32 [512, 4096], P(None, ('curve', 'level')), may hold values from -6 to 6
- counts: int32 [32], replicated, may hold values from 96 to 128, as said below
- neighbours: int32 [6, 4096], P(None, ('curve', 'level')), may hold values from -1 to 4095, as said below
Outputs:
- solution: float32 [512, 4096], P(None, ('curve', 'level'))
- residual: float32 [512, 4096], P(None, ('curve', 'level'))
- residual_norm: float32 [], replicated
Inputs may be any that keep to these rules, and one draw needn't show every extreme that they name: `counts`: some device holds 128 live bricks and some device holds 96. `neighbours`: A slot's global number is its device times 128 plus its position. The relation is symmetric across opposite faces; padding slots have -1 on every face and no brick names them. Live bricks are numbered along the curve; the brick across face 0, 2 or 4 lies earlier on the curve and the one across face 1, 3 or 5 later, at most 256 live bricks away.
All inputs are finite; a program needn't handle non-finite values.
Results may differ from a plain program's by a relative error of at most 0.00027.
Values sent between devices are 32-bit elements; how exact they have to be, the bound alone decides.
A program may use at most 64 MiB of HBM per device.

v0:
```python
import functools

import jax
import jax.numpy as jnp
from jax import lax
from jax.experimental import pallas as pl
from jax.experimental.pallas import tpu as pltpu
from jax.sharding import PartitionSpec as P

MIN_LIVE = 96
LAYER = 256
HOPS = 3
AXES = ("curve", "level")
MESH = pl.DeviceIdType.MESH
RELAXATION = 2.0 / 3.0
RELAX_FINE = RELAXATION / 6.0
RELAX_COARSE = RELAXATION / 1.5
F32 = jnp.float32


def kernel(
    sizes,
    stages,
    right_ref,
    counts_ref,
    neighbours_ref,
    solution_ref,
    residual_ref,
    norm_ref,
    source,
    first,
    second,
    image,
    zghost,
    paired,
    coarse,
    shifted,
    doubled,
    held,
    applied_ref,
    faces_fine,
    packed_fine,
    windows_fine,
    faces_coarse,
    packed_coarse,
    windows_coarse,
    sums,
    *sems,
):
    link_sems, relay_sems, pair_sems, far_sems, (sum_send, sum_recv) = [
        sems[i : i + 2] for i in range(0, 10, 2)
    ]
    curve_size, level_size = sizes
    total = curve_size * level_size
    me = lax.axis_index("curve") * level_size + lax.axis_index("level")
    lanes = right_ref.shape[1]
    half = lanes // 2

    def place(index):
        return (index // level_size, index % level_size)

    barrier = pltpu.get_barrier_semaphore()
    greeted = 0
    for size, _, peer in stages:
        for k in range(1, size):
            pl.semaphore_signal(barrier, inc=1, device_id=peer(k), device_id_type=MESH)
            greeted += 1
    direct = len(stages) == 1
    if not direct:
        for hop in range(1, HOPS + 1):
            for sign in (1, -1):
                target = (me + sign * hop + total) % total
                pl.semaphore_signal(barrier, inc=1, device_id=place(target), device_id_type=MESH)
                greeted += 1

    lane = lax.broadcasted_iota(jnp.int32, (1, lanes), 1)
    own_count = counts_ref[me]
    live = lane < own_count
    for x in range(8):
        rows = pl.ds(64 * x, 64)
        value = jnp.where(live, right_ref[rows, :], 0.0)
        source[rows, :] = value
        first[rows, :] = RELAX_FINE * value

    nb = neighbours_ref[...]
    present = nb >= 0
    owner = nb // lanes
    offset = nb % lanes
    face_id = lax.broadcasted_iota(jnp.int32, nb.shape, 0)
    hop_of = jnp.where(face_id % 2 == 0, me - owner, owner - me)
    hop_of = jnp.where(present, hop_of, -1)
    far_count = counts_ref[jnp.maximum(me - HOPS, 0)]
    odd = me % 2
    even = 1 - odd
    partner = me + 1 - 2 * odd
    earlier_pair = me >= 2
    later_pair = me - odd + 2 < total
    reaches = (1 + 2 * even, 1 + 2 * odd)
    arrives = (2 * odd, 2 * even)
    far_there = jnp.where(odd == 1, me + HOPS < total, me >= HOPS)
    far_device = (me + HOPS * (2 * odd - 1) + total) % total
    skipped = jnp.where(
        (face_id % 2 == 0) & (hop_of == HOPS), even * (far_count - half), 0
    )
    where_at = jnp.clip(offset - skipped, 0, lanes - 1)
    low_half = jnp.broadcast_to(lane < half, (8, lanes))
    pack_index = jnp.broadcast_to(odd * (own_count - half) + lane % half, (8, lanes))

    def pick(block, index):
        return jnp.take_along_axis(block, index, axis=1, mode="promise_in_bounds")

    finishing = []

    def send(src, dst, sems, at, target, sends):
        made = pltpu.make_async_remote_copy(
            src_ref=src,
            dst_ref=dst,
            send_sem=sems[0].at[at],
            recv_sem=sems[1].at[at],
            device_id=place(target),
            device_id_type=MESH,
        )
        finishing.append((made, sends))
        return made

    def exchange(stage, values, extent, faces, packed, windows, meanwhile):
        area = extent * extent
        last = extent - 1
        pack = 3 * area // 2
        for direction in (0, 1):
            at = last if direction == 0 else 0
            faces[direction, 0:area, :] = values[pl.ds(at * area, area), :]
            for x in range(extent):
                faces[direction, pl.ds(area + x * extent, extent), :] = values[
                    pl.ds(x * area + at * extent, extent), :
                ]
            faces[direction, pl.ds(2 * area, area), :] = values[pl.ds(at, area, extent), :]
        if stage == 0:
            pl.semaphore_wait(barrier, greeted)
        links = []
        for chunk in range(3):
            rows = pl.ds(chunk * area, area)
            for direction in (0, 1):
                reach = reaches[direction]
                target = me + reach if direction == 0 else me - reach
                made = send(
                    faces.at[direction, rows],
                    windows.at[direction, reach - 1, rows],
                    link_sems,
                    (stage, direction, chunk),
                    (target + total) % total,
                    later_pair if direction == 0 else earlier_pair,
                )
                pl.when(later_pair if direction == 0 else earlier_pair)(made.start)
                links.append((direction, chunk, rows, made))
        inside = send(faces.at[odd], windows.at[odd, 0], pair_sems, (stage,), partner, None)
        inside.start()
        for r in range(0, pack, 8):
            a = pick(faces[1 - odd, pl.ds(r, 8), :], pack_index)
            b = pick(faces[1 - odd, pl.ds(pack + r, 8), :], pack_index)
            packed[pl.ds(r, 8), :] = jnp.where(low_half, a, b)
        far = send(
            packed, windows.at[1 - odd, 2, pl.ds(0, pack)], far_sems, (stage,), far_device, far_there
        )
        pl.when(far_there)(far.start)
        def ghost(face, hops_in, blocks):
            direction, slot = face % 2, face // 2
            at = jnp.broadcast_to(where_at[face : face + 1, :], (8, lanes))
            is_packed = odd == direction
            at_high = jnp.where(is_packed, jnp.minimum(at + half, lanes - 1), at)
            hops = jnp.broadcast_to(hop_of[face : face + 1, :], (8, lanes))
            pieces = []
            for r in range(0, area, 8):
                row = slot * area + r
                block = blocks[r // 8]
                for hop in hops_in:
                    index = at
                    if hop == 0:
                        window = faces[direction, pl.ds(row, 8), :]
                    elif hop < HOPS or row < pack:
                        window = windows[direction, hop - 1, pl.ds(row, 8), :]
                    else:
                        start = pl.multiple_of(row - jnp.where(is_packed, pack, 0), 8)
                        window = windows[direction, hop - 1, pl.ds(start, 8), :]
                        index = at_high
                    block = jnp.where(hops == hop, pick(window, index), block)
                pieces.append(block)
            return pieces

        empty = [jnp.zeros((8, lanes), F32)] * (area // 8)
        for face in range(6):
            for r, block in enumerate(ghost(face, (0,), empty)):
                held[face, pl.ds(8 * r, 8), :] = block
        meanwhile()
        relays = []
        for direction, chunk, rows, made in links:
            comes = earlier_pair if direction == 0 else later_pair
            relay = send(
                windows.at[direction, arrives[direction], rows],
                windows.at[direction, 1, rows],
                relay_sems,
                (stage, direction, chunk),
                partner,
                comes,
            )

            @pl.when(comes)
            def _():
                made.wait_recv()
                relay.start()

            relays.append((relay, comes))
        inside.wait_recv()
        pl.when(far_there)(far.wait_recv)
        ghosts = []
        for face in range(6):
            relay, comes = relays[face]
            pl.when(comes)(relay.wait_recv)
            blocks = [held[face, pl.ds(r, 8), :] for r in range(0, area, 8)]
            ghosts.append(jnp.concatenate(ghost(face, (1, 2, 3), blocks), axis=0))
        return ghosts

    zrow = lax.broadcasted_iota(jnp.int32, (8, 8, lanes), 1)

    zghost[...] = jnp.zeros_like(zghost)

    def inner(values):
        for x in range(8):
            rows = pl.ds(64 * x, 64)
            here = values[rows, :]
            edge = jnp.zeros((8, lanes), F32)
            beside = jnp.concatenate([edge, here[:-8]], axis=0) + jnp.concatenate(
                [here[8:], edge], axis=0
            )
            if x > 0:
                beside = beside + values[pl.ds(64 * (x - 1), 64), :]
            if x < 7:
                beside = beside + values[pl.ds(64 * (x + 1), 64), :]
            cube = here.reshape(8, 8, lanes)
            below = jnp.where(zrow == 0, 0.0, pltpu.roll(cube, 1, 1))
            above = jnp.where(zrow == 7, 0.0, pltpu.roll(cube, 7, 1))
            beside = beside + (below + above).reshape(64, lanes)
            applied_ref[rows, :] = 6.0 * here - beside

    def fine(values, ghosts, use):
        g0, g1, g2, g3, g4, g5 = ghosts
        zghost[pl.ds(0, 64, 8), :] = g4
        zghost[pl.ds(7, 64, 8), :] = g5
        for x in range(8):
            rows = pl.ds(64 * x, 64)
            applied = applied_ref[rows, :] - zghost[rows, :]
            if x == 0:
                applied = applied - g0
            if x == 7:
                applied = applied - g1
            applied = jnp.concatenate(
                [
                    applied[:8] - g2[8 * x : 8 * x + 8],
                    applied[8:56],
                    applied[56:] - g3[8 * x : 8 * x + 8],
                ],
                axis=0,
            )
            use(x, rows, values[rows, :], applied)

    def exchange_fine(stage, k, values):
        return exchange(
            stage,
            values,
            8,
            faces_fine.at[k],
            packed_fine.at[k],
            windows_fine.at[k],
            lambda: inner(values),
        )

    def exchange_coarse(stage, k, meanwhile):
        return exchange(
            stage,
            coarse,
            4,
            faces_coarse.at[k],
            packed_coarse.at[k],
            windows_coarse.at[k],
            meanwhile,
        )

    def sweep(x, rows, here, applied):
        second[rows, :] = here + RELAX_FINE * (source[rows, :] - applied)

    fine(first, exchange_fine(0, 0, first), sweep)

    slabs = []

    def restrict(x, rows, here, applied):
        slabs.append(source[rows, :] - applied)
        if x % 2 == 1:
            both = slabs[x - 1] + slabs[x]
            for y in range(4):
                paired[pl.ds(32 * (x // 2) + 8 * y, 8), :] = (
                    both[16 * y : 16 * y + 8] + both[16 * y + 8 : 16 * y + 16]
                )

    ghosts = exchange_fine(1, 1, second)
    fine(second, ghosts, restrict)
    coarse_rhs = 0.125 * (paired[pl.ds(0, 64, 2), :] + paired[pl.ds(1, 64, 2), :])
    coarse_one = RELAX_COARSE * coarse_rhs
    coarse[...] = coarse_one
    g0, g1, g2, g3, g4, g5 = exchange_coarse(2, 0, lambda: None)
    beside = jnp.concatenate([g0, coarse_one[:-16]], axis=0) + jnp.concatenate(
        [coarse_one[16:], g1], axis=0
    )
    for k, shift in enumerate((4, 60, 1, 63)):
        shifted[k, :, :] = pltpu.roll(coarse_one, shift, 0)
    for x in range(4):
        shifted[0, pl.ds(16 * x, 4), :] = g2[4 * x : 4 * x + 4]
        shifted[1, pl.ds(16 * x + 12, 4), :] = g3[4 * x : 4 * x + 4]
    for x in range(4):
        for y in range(4):
            at = 16 * x + 4 * y
            shifted[2, pl.ds(at, 1), :] = g4[4 * x + y : 4 * x + y + 1]
            shifted[3, pl.ds(at + 3, 1), :] = g5[4 * x + y : 4 * x + y + 1]
    beside = beside + (shifted[0] + shifted[1]) + (shifted[2] + shifted[3])
    coarse_two = coarse_one + RELAX_COARSE * (coarse_rhs - 0.25 * (6.0 * coarse_one - beside))
    coarse[...] = coarse_two
    paired[pl.ds(0, 64, 2), :] = coarse_two
    paired[pl.ds(1, 64, 2), :] = coarse_two

    def correct():
        for x in range(8):
            for y in range(8):
                rows = pl.ds(64 * x + 8 * y, 8)
                lift = paired[pl.ds(32 * (x // 2) + 8 * (y // 2), 8), :]
                second[rows, :] = second[rows, :] + lift
        inner(second)

    corrections = exchange_coarse(3, 1, correct)
    for face in range(6):
        doubled[face, pl.ds(0, 16, 2), :] = corrections[face]
        doubled[face, pl.ds(1, 16, 2), :] = corrections[face]
        ghosts[face] = ghosts[face] + jnp.concatenate(
            [doubled[face, pl.ds(8 * (a // 2), 8), :] for a in range(8)], axis=0
        )

    def smooth(x, rows, here, applied):
        first[rows, :] = here + RELAX_FINE * (source[rows, :] - applied)

    fine(second, ghosts, smooth)

    parts = [jnp.zeros((8, lanes), F32)] * 5

    def fold(block):
        return jnp.sum(block.reshape(8, 8, lanes), axis=0)

    def finish(x, rows, here, applied):
        image[rows, :] = applied
        r = source[rows, :]
        for k, term in enumerate((r * here, here * applied, r * r, r * applied, applied * applied)):
            parts[k] = parts[k] + fold(term)

    fine(first, exchange_fine(4, 2, first), finish)

    tile = jnp.zeros((1, lanes), F32)
    for k in range(5):
        one = jnp.sum(jnp.sum(parts[k], axis=0, keepdims=True), axis=1, keepdims=True)
        tile = jnp.where(lane == k, one, tile)
    base = 0
    for size, mine, peer in stages:
        sums[base + mine] = tile
        copies = []
        for k in range(1, size):
            made = pltpu.make_async_remote_copy(
                src_ref=sums.at[base + mine],
                dst_ref=sums.at[base + mine],
                send_sem=sum_send.at[base + k],
                recv_sem=sum_recv.at[base + k],
                device_id=peer(k),
                device_id_type=MESH,
            )
            made.start()
            copies.append(made)
        for made in copies:
            made.wait_recv()
        tile = jnp.sum(sums[base : base + size], axis=0)
        for made in copies:
            made.wait_send()
        base += size
    along, curvature, old_square, cross, image_square = [
        jnp.sum(jnp.where(lane == k, tile, 0.0), axis=1, keepdims=True) for k in range(5)
    ]
    step = along / curvature
    square = old_square - 2.0 * step * cross + step * step * image_square
    norm_ref[0] = jnp.sqrt(square)[0, 0]
    for x in range(8):
        rows = pl.ds(64 * x, 64)
        solution_ref[rows, :] = step * first[rows, :]
        residual_ref[rows, :] = source[rows, :] - step * image[rows, :]
    for made, sends in finishing:
        if sends is None:
            made.wait_send()
        else:
            pl.when(sends)(made.wait_send)


def local(sizes, right_side, counts, neighbours):
    cells, lanes = right_side.shape
    curve_size, level_size = sizes
    total = curve_size * level_size

    def body(*refs):
        curve, level = lax.axis_index("curve"), lax.axis_index("level")
        if total <= 64:
            me = curve * level_size + level

            def everyone(k):
                other = (me + k) % total
                return (other // level_size, other % level_size)

            stages = [(total, me, everyone)]
        else:
            stages = [
                (level_size, level, lambda k: (curve, (level + k) % level_size)),
                (curve_size, curve, lambda k: ((curve + k) % curve_size, level)),
            ]
        kernel(sizes, stages, *refs)

    sum_rows = total if total <= 64 else curve_size + level_size
    vmem = pl.BlockSpec(memory_space=pltpu.VMEM)
    block = jax.ShapeDtypeStruct((cells, lanes), F32)
    out = pl.pallas_call(
        body,
        out_shape=(block, block, jax.ShapeDtypeStruct((1,), F32)),
        in_specs=[vmem, pl.BlockSpec(memory_space=pltpu.SMEM), vmem],
        out_specs=(vmem, vmem, pl.BlockSpec(memory_space=pltpu.SMEM)),
        scratch_shapes=[
            pltpu.VMEM((cells, lanes), F32),
            pltpu.VMEM((cells, lanes), F32),
            pltpu.VMEM((cells, lanes), F32),
            pltpu.VMEM((cells, lanes), F32),
            pltpu.VMEM((cells, lanes), F32),
            pltpu.VMEM((cells // 4, lanes), F32),
            pltpu.VMEM((cells // 8, lanes), F32),
            pltpu.VMEM((4, cells // 8, lanes), F32),
            pltpu.VMEM((6, 32, lanes), F32),
            pltpu.VMEM((6, 64, lanes), F32),
            pltpu.VMEM((cells, lanes), F32),
            pltpu.VMEM((3, 2, 192, lanes), F32),
            pltpu.VMEM((3, 96, lanes), F32),
            pltpu.VMEM((3, 2, HOPS, 192, lanes), F32),
            pltpu.VMEM((2, 2, 48, lanes), F32),
            pltpu.VMEM((2, 24, lanes), F32),
            pltpu.VMEM((2, 2, HOPS, 48, lanes), F32),
            pltpu.VMEM((sum_rows, 1, lanes), F32),
            pltpu.SemaphoreType.DMA((5, 2, 3)),
            pltpu.SemaphoreType.DMA((5, 2, 3)),
            pltpu.SemaphoreType.DMA((5, 2, 3)),
            pltpu.SemaphoreType.DMA((5, 2, 3)),
            pltpu.SemaphoreType.DMA((5,)),
            pltpu.SemaphoreType.DMA((5,)),
            pltpu.SemaphoreType.DMA((5,)),
            pltpu.SemaphoreType.DMA((5,)),
            pltpu.SemaphoreType.DMA((sum_rows,)),
            pltpu.SemaphoreType.DMA((sum_rows,)),
        ],
        compiler_params=pltpu.CompilerParams(collective_id=0, has_side_effects=True),
    )(right_side, counts, neighbours)
    return out[0], out[1], out[2].reshape(())


def solution(mesh):
    sizes = tuple(mesh.shape[name] for name in AXES)
    in_specs = (P(None, AXES), P(), P(None, AXES))
    out_specs = (P(None, AXES), P(None, AXES), P())
    return jax.shard_map(
        functools.partial(local, sizes), mesh=mesh, in_specs=in_specs, out_specs=out_specs, check_vma=False
    )
```

profile of v0, /device:TPU:0, one launch (start us, length us, event | category | flops | bytes accessed | tf_op | source)
XLA Modules:
  0.0 49.0 jit_solution(3298402295431870543)
XLA Ops:
  0.6 44.2 %shard_map.58 = (f32[512,128]{1,0:T(8,128)}, f32[512,128]{1,0:T(8,128)}, f32[1]{0:T(128)}) custom-call(f32[512,128]{1,0:T(8,128)} %refs_0_.1, s32[32]{0:T(128)} %refs_1_.1, s32[6,128]{1,0:T(8,128)} %refs_2_.1), custom_call_target="tpu_custom_call" | custom-call | tf_op jit(solution)/shard_map/pallas_call | solution.py:430
  44.8 0.0 copy-start
  44.8 1.7 %copy.9 = f32[512,128]{1,0:T(8,128)} copy(f32[512,128]{1,0:T(8,128)} %get-tuple-element.12) | data formatting | bytes 524288
  46.5 0.0 copy-done
  46.5 0.7 %copy.10 = f32[512,128]{1,0:T(8,128)} copy(f32[512,128]{1,0:T(8,128)S(1)} %copy-done) | data formatting | bytes 524288
Async XLA Ops:
  44.8 1.7 %copy-start = (f32[512,128]{1,0:T(8,128)S(1)}, f32[512,128]{1,0:T(8,128)}, u32[]{:S(2)}) copy-start(f32[512,128]{1,0:T(8,128)} %get-tuple-element.13) | copy-start | bytes 786436
where the time goes:
time: 49.2 us; the launch traced here: 49 us
  Pallas kernels  44.2 us (90%)
  local copies, waits for them, and re-layouts  2.42 us (5%)
  between operations  2.41 us (5%)
    pallas_call x1, Pallas kernels, local(): pl.pallas_call(body, out_shape=(block, block, jax.ShapeDtypeStruct((1,),...  44.2 us
    unnamed x4, local copies, waits for them, and re-layouts  2.42 us

commit v1 on v0

--- a/solution.py
+++ b/solution.py
@@ -10,6 +10,7 @@
 MIN_LIVE = 96
 LAYER = 256
 HOPS = 3
+PIECES = 2
 AXES = ("curve", "level")
 MESH = pl.DeviceIdType.MESH
 RELAXATION = 2.0 / 3.0
@@ -24,13 +25,11 @@
     right_ref,
     counts_ref,
     neighbours_ref,
-    solution_ref,
-    residual_ref,
-    norm_ref,
+    first,
+    image,
     source,
-    first,
+    tile_ref,
     second,
-    image,
     zghost,
     paired,
     coarse,
@@ -385,21 +384,36 @@
         for made in copies:
             made.wait_send()
         base += size
-    along, curvature, old_square, cross, image_square = [
-        jnp.sum(jnp.where(lane == k, tile, 0.0), axis=1, keepdims=True) for k in range(5)
-    ]
-    step = along / curvature
-    square = old_square - 2.0 * step * cross + step * step * image_square
-    norm_ref[0] = jnp.sqrt(square)[0, 0]
-    for x in range(8):
-        rows = pl.ds(64 * x, 64)
-        solution_ref[rows, :] = step * first[rows, :]
-        residual_ref[rows, :] = source[rows, :] - step * image[rows, :]
+    tile_ref[...] = tile
     for made, sends in finishing:
         if sends is None:
             made.wait_send()
         else:
             pl.when(sends)(made.wait_send)
+
+
+def finish(p_ref, image_ref, source_ref, tile_ref, sol_hbm, res_hbm, norm_ref, sol, res, sems):
+    lanes = p_ref.shape[1]
+    rows_per = p_ref.shape[0] // PIECES
+    lane = lax.broadcasted_iota(jnp.int32, (1, lanes), 1)
+    tile = tile_ref[...]
+    along, curvature, old_square, cross, image_square = [
+        jnp.sum(jnp.where(lane == k, tile, 0.0), axis=1, keepdims=True) for k in range(5)
+    ]
+    step = along / curvature
+    copies = []
+    for x in range(PIECES):
+        rows = pl.ds(rows_per * x, rows_per)
+        sol[rows, :] = step * p_ref[rows, :]
+        res[rows, :] = source_ref[rows, :] - step * image_ref[rows, :]
+        for k, (here, there) in enumerate(((sol, sol_hbm), (res, res_hbm))):
+            made = pltpu.make_async_copy(here.at[rows], there.at[rows], sems.at[k, x])
+            made.start()
+            copies.append(made)
+    square = old_square - 2.0 * step * cross + step * step * image_square
+    norm_ref[0] = jnp.sqrt(square)[0, 0]
+    for made in copies:
+        made.wait()
 
 
 def local(sizes, right_side, counts, neighbours):
@@ -427,15 +441,13 @@
     sum_rows = total if total <= 64 else curve_size + level_size
     vmem = pl.BlockSpec(memory_space=pltpu.VMEM)
     block = jax.ShapeDtypeStruct((cells, lanes), F32)
+    whole = pltpu.VMEM((cells, lanes), F32)
     out = pl.pallas_call(
         body,
-        out_shape=(block, block, jax.ShapeDtypeStruct((1,), F32)),
+        out_shape=(whole, whole, whole, pltpu.VMEM((1, lanes), F32)),
         in_specs=[vmem, pl.BlockSpec(memory_space=pltpu.SMEM), vmem],
-        out_specs=(vmem, vmem, pl.BlockSpec(memory_space=pltpu.SMEM)),
+        out_specs=(vmem,) * 4,
         scratch_shapes=[
-            pltpu.VMEM((cells, lanes), F32),
-            pltpu.VMEM((cells, lanes), F32),
-            pltpu.VMEM((cells, lanes), F32),
             pltpu.VMEM((cells, lanes), F32),
             pltpu.VMEM((cells, lanes), F32),
             pltpu.VMEM((cells // 4, lanes), F32),
@@ -464,6 +476,18 @@
         ],
         compiler_params=pltpu.CompilerParams(collective_id=0, has_side_effects=True),
     )(right_side, counts, neighbours)
+    hbm = pl.BlockSpec(memory_space=pl.ANY)
+    out = pl.pallas_call(
+        finish,
+        out_shape=(block, block, jax.ShapeDtypeStruct((1,), F32)),
+        in_specs=[vmem] * 4,
+        out_specs=(hbm, hbm, pl.BlockSpec(memory_space=pltpu.SMEM)),
+        scratch_shapes=[
+            pltpu.VMEM((cells, lanes), F32),
+            pltpu.VMEM((cells, lanes), F32),
+            pltpu.SemaphoreType.DMA((2, PIECES)),
+        ],
+    )(*[pltpu.with_memory_space_constraint(a, pltpu.VMEM) for a in out])
     return out[0], out[1], out[2].reshape(())
 
 

time: 49.2 us -> 45.4 us (0.923)
  local copies, waits for them, and re-layouts: 2.42 us -> 0 us
  between operations: 2.41 us -> 0.64 us
    unnamed x4 -> x0, local copies, waits for them, and re-layouts: 2.42 us -> none
    pallas_call x1 -> x2, Pallas kernels: 44.2 us -> 44.6 us  [the longest x1 43.2 us: local(): pl.pallas_call(body, out_shape=(whole, whole, whole, pltpu.VMEM((1, lanes...]
where the time goes in v1:
time: 45.4 us; the launch traced here: 45.3 us
  Pallas kernels  44.6 us (98%)
  between operations  0.64 us (1%)
    pallas_call x1, Pallas kernels, local(): pl.pallas_call(body, out_shape=(whole, whole, whole, pltpu.VMEM((1, lanes...  43.2 us
    pallas_call x1, Pallas kernels, local(): pl.pallas_call(finish, out_shape=(block, block, jax.ShapeDtypeStruct((1,)...  1.43 us

profile of v1, /device:TPU:0, one launch (start us, length us, event | category | flops | bytes accessed | tf_op | source)
XLA Modules:
  0.0 45.3 jit_solution(13226825059143284061)
XLA Ops:
  0.6 43.2 %shard_map.58 = (f32[512,128]{1,0:T(8,128)S(1)}, f32[512,128]{1,0:T(8,128)S(1)}, f32[512,128]{1,0:T(8,128)S(1)}, f32[1,128]{1,0:T(1,128)S(1)}) custom-call(f32[512,128]{1,0:T(8,128)} %refs_0_.1, s32[32]{0:T(128)} %refs_1_.1, s32[6,128]{1,0:T(8,128)} %refs_2_.1), custom_call_target="tpu_custom_call" | custom-call | tf_op jit(solution)/shard_map/pallas_call | solution.py:445
  43.9 1.4 %shard_map.59 = (f32[512,128]{1,0:T(8,128)}, f32[512,128]{1,0:T(8,128)}, f32[1]{0:T(128)}) custom-call(f32[512,128]{1,0:T(8,128)S(1)} %get-tuple-element.10.p_ref, f32[512,128]{1,0:T(8,128)S(1)} %get-tuple-element.11.image_ref, f32[512,128]{1,0:T(8,128)S(1)} %get-tuple-element.12.source_ref, f32[1,128]{1,0:T(1,128)S(1)} %get-tuple-element.13.tile_ref), custom_call_target="tpu_custom_call" | custom-call | tf_op jit(solution)/shard_map/pallas_call | solution.py:480

commit v2 on v1

v2 whole, which is shorter than its diff:
```python
import functools

import jax
import jax.numpy as jnp
from jax import lax
from jax.experimental import pallas as pl
from jax.experimental.pallas import tpu as pltpu
from jax.sharding import PartitionSpec as P

MIN_LIVE = 96
LAYER = 256
HOPS = 3
PIECES = 2
AXES = ("curve", "level")
MESH = pl.DeviceIdType.MESH
RELAXATION = 2.0 / 3.0
RELAX_FINE = RELAXATION / 6.0
RELAX_COARSE = RELAXATION / 1.5
F32 = jnp.float32


def kernel(
    sizes,
    stages,
    right_hbm,
    counts_hbm,
    neighbours_hbm,
    first,
    image,
    source,
    tile_ref,
    counts_ref,
    neighbours_ref,
    second,
    zghost,
    paired,
    halved,
    yghost_coarse,
    zghost_coarse,
    doubled,
    applied_ref,
    ghosts_fine,
    ghosts_coarse,
    faces_fine,
    packed_fine,
    windows_fine,
    faces_coarse,
    packed_coarse,
    windows_coarse,
    sums,
    loads,
    *sems,
):
    link_sems, relay_sems, pair_sems, far_sems, (sum_send, sum_recv) = [
        sems[i : i + 2] for i in range(0, 10, 2)
    ]
    curve_size, level_size = sizes
    total = curve_size * level_size
    me = lax.axis_index("curve") * level_size + lax.axis_index("level")
    lanes = source.shape[1]
    half = lanes // 2

    def place(index):
        return (index // level_size, index % level_size)

    barrier = pltpu.get_barrier_semaphore()
    greeted = 0
    if len(stages) > 1:
        for hop in range(1, HOPS + 1):
            for sign in (1, -1):
                target = (me + sign * hop + total) % total
                pl.semaphore_signal(barrier, inc=1, device_id=place(target), device_id_type=MESH)
                greeted += 1
    for size, _, peer in stages:
        for k in range(1, size):
            pl.semaphore_signal(barrier, inc=1, device_id=peer(k), device_id_type=MESH)
            greeted += 1
    inputs = [
        pltpu.make_async_copy(src, dst, loads.at[k])
        for k, (src, dst) in enumerate(
            ((right_hbm, second), (counts_hbm, counts_ref), (neighbours_hbm, neighbours_ref))
        )
    ]
    for made in inputs:
        made.start()
    zghost[...] = jnp.zeros_like(zghost)
    yghost_coarse[...] = jnp.zeros_like(yghost_coarse)
    zghost_coarse[...] = jnp.zeros_like(zghost_coarse)
    for made in inputs:
        made.wait()

    lane = lax.broadcasted_iota(jnp.int32, (1, lanes), 1)
    own_count = counts_ref[me]
    live = lane < own_count
    for x in range(8):
        rows = pl.ds(64 * x, 64)
        value = jnp.where(live, second[rows, :], 0.0)
        source[rows, :] = value
        first[rows, :] = RELAX_FINE * value

    nb = neighbours_ref[...]
    present = nb >= 0
    owner = nb // lanes
    offset = nb % lanes
    face_id = lax.broadcasted_iota(jnp.int32, nb.shape, 0)
    hop_of = jnp.where(face_id % 2 == 0, me - owner, owner - me)
    hop_of = jnp.where(present, hop_of, -1)
    far_count = counts_ref[jnp.maximum(me - HOPS, 0)]
    odd = me % 2
    even = 1 - odd
    partner = me + 1 - 2 * odd
    earlier_pair = me >= 2
    later_pair = me - odd + 2 < total
    reaches = (1 + 2 * even, 1 + 2 * odd)
    arrives = (2 * odd, 2 * even)
    far_there = jnp.where(odd == 1, me + HOPS < total, me >= HOPS)
    far_device = (me + HOPS * (2 * odd - 1) + total) % total
    skipped = jnp.where(
        (face_id % 2 == 0) & (hop_of == HOPS), even * (far_count - half), 0
    )
    where_at = jnp.clip(offset - skipped, 0, lanes - 1)
    low_half = jnp.broadcast_to(lane < half, (8, lanes))
    pack_index = jnp.broadcast_to(odd * (own_count - half) + lane % half, (8, lanes))

    def pick(block, index):
        return jnp.take_along_axis(block, index, axis=1, mode="promise_in_bounds")

    finishing = []

    def send(src, dst, sems, at, target, sends):
        made = pltpu.make_async_remote_copy(
            src_ref=src,
            dst_ref=dst,
            send_sem=sems[0].at[at],
            recv_sem=sems[1].at[at],
            device_id=place(target),
            device_id_type=MESH,
        )
        finishing.append((made, sends))
        return made

    def cut(values, extent, faces):
        area = extent * extent
        for direction in (0, 1):
            at = extent - 1 if direction == 0 else 0
            faces[direction, 0:area, :] = values[pl.ds(at * area, area), :]
            for x in range(extent):
                faces[direction, pl.ds(area + x * extent, extent), :] = values[
                    pl.ds(x * area + at * extent, extent), :
                ]
            faces[direction, pl.ds(2 * area, area), :] = values[pl.ds(at, area, extent), :]

    class Exchange:
        def __init__(self, stage, area, chunks, faces, packed, windows, ghosts):
            self.stage, self.area, self.chunks = stage, area, chunks
            self.faces, self.packed, self.windows, self.ghosts = faces, packed, windows, ghosts

        def post(self):
            faces, packed, windows, stage = self.faces, self.packed, self.windows, self.stage
            size = 3 * self.area // self.chunks
            pack = 3 * self.area // 2
            self.links = []
            for chunk in range(self.chunks):
                rows = pl.ds(chunk * size, size)
                for direction in (0, 1):
                    reach = reaches[direction]
                    target = me + reach if direction == 0 else me - reach
                    made = send(
                        faces.at[direction, rows],
                        windows.at[direction, reach - 1, rows],
                        link_sems,
                        (stage, direction, chunk),
                        (target + total) % total,
                        later_pair if direction == 0 else earlier_pair,
                    )
                    pl.when(later_pair if direction == 0 else earlier_pair)(made.start)
                    self.links.append((direction, chunk, rows, made))
            self.inside = send(
                faces.at[odd], windows.at[odd, 0], pair_sems, (stage,), partner, None
            )
            self.inside.start()
            for r in range(0, pack, 8):
                a = pick(faces[1 - odd, pl.ds(r, 8), :], pack_index)
                b = pick(faces[1 - odd, pl.ds(pack + r, 8), :], pack_index)
                packed[pl.ds(r, 8), :] = jnp.where(low_half, a, b)
            self.far = send(
                packed,
                windows.at[1 - odd, 2, pl.ds(0, pack)],
                far_sems,
                (stage,),
                far_device,
                far_there,
            )
            pl.when(far_there)(self.far.start)

        def pull(self, face, hops_in):
            area, faces, windows = self.area, self.faces, self.windows
            pack = 3 * area // 2
            direction, slot = face % 2, face // 2
            at = jnp.broadcast_to(where_at[face : face + 1, :], (8, lanes))
            is_packed = odd == direction
            at_high = jnp.where(is_packed, jnp.minimum(at + half, lanes - 1), at)
            hops = jnp.broadcast_to(hop_of[face : face + 1, :], (8, lanes))
            for r in range(0, area, 8):
                row = slot * area + r
                if 0 in hops_in:
                    block = jnp.zeros((8, lanes), F32)
                else:
                    block = self.ghosts[face, pl.ds(r, 8), :]
                for hop in hops_in:
                    index = at
                    if hop == 0:
                        window = faces[direction, pl.ds(row, 8), :]
                    elif hop < HOPS or row < pack:
                        window = windows[direction, hop - 1, pl.ds(row, 8), :]
                    else:
                        start = pl.multiple_of(row - jnp.where(is_packed, pack, 0), 8)
                        window = windows[direction, hop - 1, pl.ds(start, 8), :]
                        index = at_high
                    block = jnp.where(hops == hop, pick(window, index), block)
                self.ghosts[face, pl.ds(r, 8), :] = block

        def near(self):
            for face in range(6):
                self.pull(face, (0,))

        def forward(self):
            self.relays = {}
            for direction, chunk, rows, made in self.links:
                comes = earlier_pair if direction == 0 else later_pair
                relay = send(
                    self.windows.at[direction, arrives[direction], rows],
                    self.windows.at[direction, 1, rows],
                    relay_sems,
                    (self.stage, direction, chunk),
                    partner,
                    comes,
                )

                @pl.when(comes)
                def _():
                    made.wait_recv()
                    relay.start()

                self.relays[direction, chunk] = (relay, comes)

        def collect(self):
            self.inside.wait_recv()
            pl.when(far_there)(self.far.wait_recv)
            for face in range(6):
                waits = self.relays.pop((face % 2, face // 2), None)
                if waits is not None:
                    relay, comes = waits
                    pl.when(comes)(relay.wait_recv)
                self.pull(face, (1, 2, 3))

    def fine_exchange(k):
        return Exchange(
            k, 64, 3, faces_fine.at[k], packed_fine.at[k], windows_fine.at[k], ghosts_fine.at[k]
        )

    def coarse_exchange(k):
        return Exchange(
            3 + k,
            16,
            1,
            faces_coarse.at[k],
            packed_coarse.at[k],
            windows_coarse.at[k],
            ghosts_coarse.at[k],
        )

    zrow = lax.broadcasted_iota(jnp.int32, (8, 8, lanes), 1)

    def inner(values):
        for x in range(8):
            rows = pl.ds(64 * x, 64)
            here = values[rows, :]
            edge = jnp.zeros((8, lanes), F32)
            beside = jnp.concatenate([edge, here[:-8]], axis=0) + jnp.concatenate(
                [here[8:], edge], axis=0
            )
            if x > 0:
                beside = beside + values[pl.ds(64 * (x - 1), 64), :]
            if x < 7:
                beside = beside + values[pl.ds(64 * (x + 1), 64), :]
            cube = here.reshape(8, 8, lanes)
            below = jnp.where(zrow == 0, 0.0, pltpu.roll(cube, 1, 1))
            above = jnp.where(zrow == 7, 0.0, pltpu.roll(cube, 7, 1))
            beside = beside + (below + above).reshape(64, lanes)
            applied_ref[rows, :] = 6.0 * here - beside

    def with_ghosts(ghost, use):
        zghost[pl.ds(0, 64, 8), :] = ghost(4, 0, 64)
        zghost[pl.ds(7, 64, 8), :] = ghost(5, 0, 64)
        for x in range(8):
            rows = pl.ds(64 * x, 64)
            outer = zghost[rows, :]
            if x == 0:
                outer = outer + ghost(0, 0, 64)
            if x == 7:
                outer = outer + ghost(1, 0, 64)
            outer = jnp.concatenate(
                [
                    outer[:8] + ghost(2, 8 * x, 8),
                    outer[8:56],
                    outer[56:] + ghost(3, 8 * x, 8),
                ],
                axis=0,
            )
            use(x, rows, outer)

    def stored(ghosts):
        return lambda face, start, size: ghosts[face, pl.ds(start, size), :]

    def prolonged(k):
        def ghost(face, start, size):
            return jnp.concatenate(
                [
                    doubled[k, face, pl.ds(8 * (a // 2), 8), :]
                    for a in range(start // 8, (start + size) // 8)
                ],
                axis=0,
            )

        return ghost

    def double(k, face, value):
        doubled[k, face, pl.ds(0, 16, 2), :] = value
        doubled[k, face, pl.ds(1, 16, 2), :] = value

    def coarse_outer(ghosts):
        zghost_coarse[pl.ds(0, 16, 4), :] = ghosts[4]
        zghost_coarse[pl.ds(3, 16, 4), :] = ghosts[5]
        for x in range(4):
            yghost_coarse[pl.ds(16 * x, 4), :] = ghosts[2, pl.ds(4 * x, 4), :]
            yghost_coarse[pl.ds(16 * x + 12, 4), :] = ghosts[3, pl.ds(4 * x, 4), :]
        outer = yghost_coarse[...] + zghost_coarse[...]
        return jnp.concatenate(
            [outer[:16] + ghosts[0], outer[16:48], outer[48:] + ghosts[1]], axis=0
        )

    exchange = fine_exchange(0)
    cut(first, 8, exchange.faces)
    pl.semaphore_wait(barrier, greeted)
    exchange.post()
    exchange.near()
    inner(first)
    exchange.forward()
    exchange.collect()

    def sweep(x, rows, outer):
        second[rows, :] = first[rows, :] + RELAX_FINE * (
            source[rows, :] - applied_ref[rows, :] + outer
        )

    with_ghosts(stored(exchange.ghosts), sweep)

    smoothed = fine_exchange(1)
    sampled = coarse_exchange(0)
    cut(second, 8, smoothed.faces)
    for direction in (0, 1):
        for k in range(12):
            halved[direction, pl.ds(8 * k, 8), :] = (
                smoothed.faces[direction, pl.ds(16 * k, 8), :]
                + smoothed.faces[direction, pl.ds(16 * k + 8, 8), :]
            )
        sampled.faces[direction, :, :] = (
            halved[direction, pl.ds(0, 48, 2), :] + halved[direction, pl.ds(1, 48, 2), :]
        )
    sampled.post()
    smoothed.post()
    sampled.near()
    inner(second)
    for x in range(0, 8, 2):
        lower, upper = pl.ds(64 * x, 64), pl.ds(64 * x + 64, 64)
        both = (source[lower, :] - applied_ref[lower, :]) + (
            source[upper, :] - applied_ref[upper, :]
        )
        for y in range(4):
            paired[pl.ds(32 * (x // 2) + 8 * y, 8), :] = (
                both[16 * y : 16 * y + 8] + both[16 * y + 8 : 16 * y + 16]
            )
    inner_rhs = paired[pl.ds(0, 64, 2), :] + paired[pl.ds(1, 64, 2), :]
    smoothed.near()
    sampled.forward()
    sampled.collect()
    coarse_rhs = 0.125 * (inner_rhs + coarse_outer(sampled.ghosts))
    coarse_one = RELAX_COARSE * coarse_rhs

    exchange = coarse_exchange(1)
    coarse = halved.at[0]
    coarse[0:64, :] = coarse_one
    cut(coarse, 4, exchange.faces)
    exchange.post()
    exchange.near()
    row = lax.broadcasted_iota(jnp.int32, (64, lanes), 0)
    edge = jnp.zeros((16, lanes), F32)
    beside = jnp.concatenate([edge, coarse_one[:-16]], axis=0) + jnp.concatenate(
        [coarse_one[16:], edge], axis=0
    )
    beside = beside + jnp.where(row // 4 % 4 == 0, 0.0, pltpu.roll(coarse_one, 4, 0))
    beside = beside + jnp.where(row // 4 % 4 == 3, 0.0, pltpu.roll(coarse_one, 60, 0))
    beside = beside + jnp.where(row % 4 == 0, 0.0, pltpu.roll(coarse_one, 1, 0))
    beside = beside + jnp.where(row % 4 == 3, 0.0, pltpu.roll(coarse_one, 63, 0))
    coarse_two = coarse_one + RELAX_COARSE * (coarse_rhs - 0.25 * (6.0 * coarse_one - beside))
    smoothed.forward()
    exchange.forward()
    exchange.collect()
    coarse_two = coarse_two + (0.25 * RELAX_COARSE) * coarse_outer(exchange.ghosts)

    corrected = coarse_exchange(2)
    coarse[0:64, :] = coarse_two
    cut(coarse, 4, corrected.faces)
    corrected.post()
    corrected.near()
    paired[pl.ds(0, 64, 2), :] = coarse_two
    paired[pl.ds(1, 64, 2), :] = coarse_two
    for x in range(8):
        for y in range(8):
            rows = pl.ds(64 * x + 8 * y, 8)
            lift = paired[pl.ds(32 * (x // 2) + 8 * (y // 2), 8), :]
            second[rows, :] = second[rows, :] + lift
    inner(second)
    smoothed.collect()

    def smooth(x, rows, outer):
        first[rows, :] = second[rows, :] + RELAX_FINE * (
            source[rows, :] - applied_ref[rows, :] + outer
        )

    with_ghosts(stored(smoothed.ghosts), smooth)
    almost = fine_exchange(2)
    cut(first, 8, almost.faces)
    almost.post()
    corrected.forward()
    corrected.collect()

    edges = coarse_exchange(3)
    for direction in (0, 1):
        at = 3 if direction == 0 else 0
        along_rows, across_rows = pl.ds(4 * at, 4), pl.ds(at, 4, 4)
        lines = [(g, along_rows) for g in (2, 3, 4, 5)]
        lines += [(g, along_rows) for g in (0, 1)] + [(g, across_rows) for g in (4, 5)]
        lines += [(g, across_rows) for g in (0, 1, 2, 3)]
        for k, (g, rows) in enumerate(lines):
            edges.faces[direction, pl.ds(4 * k, 4), :] = corrected.ghosts[g, rows, :]
    edges.post()
    edges.near()
    for face in range(6):
        double(0, face, corrected.ghosts[face])
        own = corrected.faces[1 - face % 2, pl.ds(16 * (face // 2), 16), :]
        double(1, face, jnp.where(hop_of[face : face + 1, :] >= 0, own, 0.0))

    def lift(x, rows, outer):
        first[rows, :] = first[rows, :] + RELAX_FINE * outer

    with_ghosts(prolonged(0), lift)
    inner(first)
    almost.near()
    almost.forward()
    almost.collect()
    outermost = almost.ghosts
    own = prolonged(1)
    for face in range(6):
        outermost[face] = outermost[face] + RELAX_FINE * own(face, 0, 64)
    edges.forward()
    edges.collect()
    for face in range(6):
        double(0, face, RELAX_FINE * edges.ghosts[face])
        for k, rows in enumerate((pl.ds(0, 8), pl.ds(56, 8), pl.ds(0, 8, 8), pl.ds(7, 8, 8))):
            outermost[face, rows, :] = (
                outermost[face, rows, :] + doubled[0, face, pl.ds(8 * k, 8), :]
            )

    parts = [jnp.zeros((8, lanes), F32)] * 5

    def fold(block):
        return jnp.sum(block.reshape(8, 8, lanes), axis=0)

    def close(x, rows, outer):
        here = first[rows, :]
        applied = applied_ref[rows, :] - outer
        image[rows, :] = applied
        r = source[rows, :]
        for k, term in enumerate((r * here, here * applied, r * r, r * applied, applied * applied)):
            parts[k] = parts[k] + fold(term)

    with_ghosts(stored(outermost), close)

    tile = jnp.zeros((1, lanes), F32)
    for k in range(5):
        one = jnp.sum(jnp.sum(parts[k], axis=0, keepdims=True), axis=1, keepdims=True)
        tile = jnp.where(lane == k, one, tile)
    base = 0
    for size, mine, peer in stages:
        sums[base + mine] = tile
        copies = []
        for k in range(1, size):
            made = pltpu.make_async_remote_copy(
                src_ref=sums.at[base + mine],
                dst_ref=sums.at[base + mine],
                send_sem=sum_send.at[base + k],
                recv_sem=sum_recv.at[base + k],
                device_id=peer(k),
                device_id_type=MESH,
            )
            made.start()
            copies.append(made)
        for made, sends in finishing:
            if sends is None:
                made.wait_send()
            else:
                pl.when(sends)(made.wait_send)
        finishing.clear()
        for made in copies:
            made.wait_recv()
        tile = jnp.sum(sums[base : base + size], axis=0)
        for made in copies:
            made.wait_send()
        base += size
    tile_ref[...] = tile


def finish(p_ref, image_ref, source_ref, tile_ref, sol_hbm, res_hbm, norm_ref, sol, res, sems):
    lanes = p_ref.shape[1]
    rows_per = p_ref.shape[0] // PIECES
    lane = lax.broadcasted_iota(jnp.int32, (1, lanes), 1)
    tile = tile_ref[...]
    along, curvature, old_square, cross, image_square = [
        jnp.sum(jnp.where(lane == k, tile, 0.0), axis=1, keepdims=True) for k in range(5)
    ]
    step = along / curvature
    copies = []
    for x in range(PIECES):
        rows = pl.ds(rows_per * x, rows_per)
        sol[rows, :] = step * p_ref[rows, :]
        res[rows, :] = source_ref[rows, :] - step * image_ref[rows, :]
        for k, (here, there) in enumerate(((sol, sol_hbm), (res, res_hbm))):
            made = pltpu.make_async_copy(here.at[rows], there.at[rows], sems.at[k, x])
            made.start()
            copies.append(made)
    square = old_square - 2.0 * step * cross + step * step * image_square
    norm_ref[0] = jnp.sqrt(square)[0, 0]
    for made in copies:
        made.wait()


def local(sizes, right_side, counts, neighbours):
    cells, lanes = right_side.shape
    curve_size, level_size = sizes
    total = curve_size * level_size

    def body(*refs):
        curve, level = lax.axis_index("curve"), lax.axis_index("level")
        if total <= 64:
            me = curve * level_size + level

            def everyone(k):
                other = (me + k) % total
                return (other // level_size, other % level_size)

            stages = [(total, me, everyone)]
        else:
            stages = [
                (level_size, level, lambda k: (curve, (level + k) % level_size)),
                (curve_size, curve, lambda k: ((curve + k) % curve_size, level)),
            ]
        kernel(sizes, stages, *refs)

    sum_rows = total if total <= 64 else curve_size + level_size
    vmem = pl.BlockSpec(memory_space=pltpu.VMEM)
    block = jax.ShapeDtypeStruct((cells, lanes), F32)
    whole = pltpu.VMEM((cells, lanes), F32)
    out = pl.pallas_call(
        body,
        out_shape=(whole, whole, whole, pltpu.VMEM((1, lanes), F32)),
        in_specs=[pl.BlockSpec(memory_space=pl.ANY)] * 3,
        out_specs=(vmem,) * 4,
        scratch_shapes=[
            pltpu.SMEM(counts.shape, jnp.int32),
            pltpu.VMEM(neighbours.shape, jnp.int32),
            pltpu.VMEM((cells, lanes), F32),
            pltpu.VMEM((cells, lanes), F32),
            pltpu.VMEM((cells // 4, lanes), F32),
            pltpu.VMEM((2, 96, lanes), F32),
            pltpu.VMEM((cells // 8, lanes), F32),
            pltpu.VMEM((cells // 8, lanes), F32),
            pltpu.VMEM((2, 6, 32, lanes), F32),
            pltpu.VMEM((cells, lanes), F32),
            pltpu.VMEM((3, 6, 64, lanes), F32),
            pltpu.VMEM((4, 6, 16, lanes), F32),
            pltpu.VMEM((3, 2, 192, lanes), F32),
            pltpu.VMEM((3, 96, lanes), F32),
            pltpu.VMEM((3, 2, HOPS, 192, lanes), F32),
            pltpu.VMEM((4, 2, 48, lanes), F32),
            pltpu.VMEM((4, 24, lanes), F32),
            pltpu.VMEM((4, 2, HOPS, 48, lanes), F32),
            pltpu.VMEM((sum_rows, 1, lanes), F32),
            pltpu.SemaphoreType.DMA((3,)),
            pltpu.SemaphoreType.DMA((7, 2, 3)),
            pltpu.SemaphoreType.DMA((7, 2, 3)),
            pltpu.SemaphoreType.DMA((7, 2, 3)),
            pltpu.SemaphoreType.DMA((7, 2, 3)),
            pltpu.SemaphoreType.DMA((7,)),
            pltpu.SemaphoreType.DMA((7,)),
            pltpu.SemaphoreType.DMA((7,)),
            pltpu.SemaphoreType.DMA((7,)),
            pltpu.SemaphoreType.DMA((sum_rows,)),
            pltpu.SemaphoreType.DMA((sum_rows,)),
        ],
        compiler_params=pltpu.CompilerParams(collective_id=0, has_side_effects=True),
    )(right_side, counts, neighbours)
    hbm = pl.BlockSpec(memory_space=pl.ANY)
    out = pl.pallas_call(
        finish,
        out_shape=(block, block, jax.ShapeDtypeStruct((1,), F32)),
        in_specs=[vmem] * 4,
        out_specs=(hbm, hbm, pl.BlockSpec(memory_space=pltpu.SMEM)),
        scratch_shapes=[
            pltpu.VMEM((cells, lanes), F32),
            pltpu.VMEM((cells, lanes), F32),
            pltpu.SemaphoreType.DMA((2, PIECES)),
        ],
    )(*[pltpu.with_memory_space_constraint(a, pltpu.VMEM) for a in out])
    return out[0], out[1], out[2].reshape(())


def solution(mesh):
    sizes = tuple(mesh.shape[name] for name in AXES)
    in_specs = (P(None, AXES), P(), P(None, AXES))
    out_specs = (P(None, AXES), P(None, AXES), P())
    return jax.shard_map(
        functools.partial(local, sizes), mesh=mesh, in_specs=in_specs, out_specs=out_specs, check_vma=False
    )
```

time: 45.4 us -> 42.2 us (0.930)
  Pallas kernels: 44.6 us -> 41.4 us
    pallas_call x1, Pallas kernels: 43.2 us -> 40 us  [local(): pl.pallas_call(body, out_shape=(whole, whole, whole, pltpu.VMEM((1, lanes...]
where the time goes in v2:
time: 42.2 us; the launch traced here: 42.1 us
  Pallas kernels  41.4 us (98%)
  between operations  0.64 us (2%)
    pallas_call x1, Pallas kernels, local(): pl.pallas_call(body, out_shape=(whole, whole, whole, pltpu.VMEM((1, lanes...  40 us
    pallas_call x1, Pallas kernels, local(): pl.pallas_call(finish, out_shape=(block, block, jax.ShapeDtypeStruct((1,)...  1.43 us

profile of v2, /device:TPU:0, one launch (start us, length us, event | category | flops | bytes accessed | tf_op | source)
XLA Modules:
  0.0 42.1 jit_solution(14982012583728213773)
XLA Ops:
  0.6 40.0 %shard_map.58 = (f32[512,128]{1,0:T(8,128)S(1)}, f32[512,128]{1,0:T(8,128)S(1)}, f32[512,128]{1,0:T(8,128)S(1)}, f32[1,128]{1,0:T(1,128)S(1)}) custom-call(f32[512,128]{1,0:T(8,128)} %refs_0_.1, s32[32]{0:T(128)} %refs_1_.1, s32[6,128]{1,0:T(8,128)} %refs_2_.1), custom_call_target="tpu_custom_call" | custom-call | tf_op jit(solution)/shard_map/pallas_call | solution.py:575
  40.6 1.4 %shard_map.59 = (f32[512,128]{1,0:T(8,128)}, f32[512,128]{1,0:T(8,128)}, f32[1]{0:T(128)}) custom-call(f32[512,128]{1,0:T(8,128)S(1)} %get-tuple-element.10.p_ref, f32[512,128]{1,0:T(8,128)S(1)} %get-tuple-element.11.image_ref, f32[512,128]{1,0:T(8,128)S(1)} %get-tuple-element.12.source_ref, f32[1,128]{1,0:T(1,128)S(1)} %get-tuple-element.13.tile_ref), custom_call_target="tpu_custom_call" | custom-call | tf_op jit(solution)/shard_map/pallas_call | solution.py:615

commit v3 on v2

--- a/solution.py
+++ b/solution.py
@@ -63,6 +63,14 @@
     def place(index):
         return (index // level_size, index % level_size)
 
+    inputs = [
+        pltpu.make_async_copy(src, dst, loads.at[k])
+        for k, (src, dst) in enumerate(
+            ((right_hbm, second), (counts_hbm, counts_ref), (neighbours_hbm, neighbours_ref))
+        )
+    ]
+    for made in inputs:
+        made.start()
     barrier = pltpu.get_barrier_semaphore()
     greeted = 0
     if len(stages) > 1:
@@ -75,14 +83,6 @@
         for k in range(1, size):
             pl.semaphore_signal(barrier, inc=1, device_id=peer(k), device_id_type=MESH)
             greeted += 1
-    inputs = [
-        pltpu.make_async_copy(src, dst, loads.at[k])
-        for k, (src, dst) in enumerate(
-            ((right_hbm, second), (counts_hbm, counts_ref), (neighbours_hbm, neighbours_ref))
-        )
-    ]
-    for made in inputs:
-        made.start()
     zghost[...] = jnp.zeros_like(zghost)
     yghost_coarse[...] = jnp.zeros_like(yghost_coarse)
     zghost_coarse[...] = jnp.zeros_like(zghost_coarse)
@@ -493,31 +493,28 @@
         one = jnp.sum(jnp.sum(parts[k], axis=0, keepdims=True), axis=1, keepdims=True)
         tile = jnp.where(lane == k, one, tile)
     base = 0
-    for size, mine, peer in stages:
+    for stage, (size, mine, peer) in enumerate(stages):
         sums[base + mine] = tile
-        copies = []
         for k in range(1, size):
             made = pltpu.make_async_remote_copy(
                 src_ref=sums.at[base + mine],
                 dst_ref=sums.at[base + mine],
-                send_sem=sum_send.at[base + k],
-                recv_sem=sum_recv.at[base + k],
+                send_sem=sum_send.at[stage],
+                recv_sem=sum_recv.at[stage],
                 device_id=peer(k),
                 device_id_type=MESH,
             )
             made.start()
-            copies.append(made)
+        arriving = sums.at[pl.ds(base, size - 1)]
         for made, sends in finishing:
             if sends is None:
                 made.wait_send()
             else:
                 pl.when(sends)(made.wait_send)
         finishing.clear()
-        for made in copies:
-            made.wait_recv()
+        pltpu.make_async_copy(arriving, arriving, sum_send.at[stage]).wait()
+        pltpu.make_async_copy(arriving, arriving, sum_recv.at[stage]).wait()
         tile = jnp.sum(sums[base : base + size], axis=0)
-        for made in copies:
-            made.wait_send()
         base += size
     tile_ref[...] = tile
 
@@ -606,8 +603,8 @@
             pltpu.SemaphoreType.DMA((7,)),
             pltpu.SemaphoreType.DMA((7,)),
             pltpu.SemaphoreType.DMA((7,)),
-            pltpu.SemaphoreType.DMA((sum_rows,)),
-            pltpu.SemaphoreType.DMA((sum_rows,)),
+            pltpu.SemaphoreType.DMA((2,)),
+            pltpu.SemaphoreType.DMA((2,)),
         ],
         compiler_params=pltpu.CompilerParams(collective_id=0, has_side_effects=True),
     )(right_side, counts, neighbours)

time: 42.2 us -> 41.6 us (0.986)
  Pallas kernels: 41.4 us -> 40.8 us
    pallas_call x1, Pallas kernels: 40 us -> 39.4 us  [local(): pl.pallas_call(body, out_shape=(whole, whole, whole, pltpu.VMEM((1, lanes...]
where the time goes in v3:
time: 41.6 us; the launch traced here: 41.4 us
  Pallas kernels  40.8 us (98%)
  between operations  0.64 us (2%)
    pallas_call x1, Pallas kernels, local(): pl.pallas_call(body, out_shape=(whole, whole, whole, pltpu.VMEM((1, lanes...  39.4 us
    pallas_call x1, Pallas kernels, local(): pl.pallas_call(finish, out_shape=(block, block, jax.ShapeDtypeStruct((1,)...  1.43 us

profile of v3, /device:TPU:0, one launch (start us, length us, event | category | flops | bytes accessed | tf_op | source)
XLA Modules:
  0.0 41.4 jit_solution(16071866391942498019)
XLA Ops:
  0.6 39.4 %shard_map.58 = (f32[512,128]{1,0:T(8,128)S(1)}, f32[512,128]{1,0:T(8,128)S(1)}, f32[512,128]{1,0:T(8,128)S(1)}, f32[1,128]{1,0:T(1,128)S(1)}) custom-call(f32[512,128]{1,0:T(8,128)} %refs_0_.1, s32[32]{0:T(128)} %refs_1_.1, s32[6,128]{1,0:T(8,128)} %refs_2_.1), custom_call_target="tpu_custom_call" | custom-call | tf_op jit(solution)/shard_map/pallas_call | solution.py:572
  40.0 1.4 %shard_map.59 = (f32[512,128]{1,0:T(8,128)}, f32[512,128]{1,0:T(8,128)}, f32[1]{0:T(128)}) custom-call(f32[512,128]{1,0:T(8,128)S(1)} %get-tuple-element.10.p_ref, f32[512,128]{1,0:T(8,128)S(1)} %get-tuple-element.11.image_ref, f32[512,128]{1,0:T(8,128)S(1)} %get-tuple-element.12.source_ref, f32[1,128]{1,0:T(1,128)S(1)} %get-tuple-element.13.tile_ref), custom_call_target="tpu_custom_call" | custom-call | tf_op jit(solution)/shard_map/pallas_call | solution.py:612

commit v4 on v3

--- a/solution.py
+++ b/solution.py
@@ -22,6 +22,7 @@
 def kernel(
     sizes,
     stages,
+    group_size,
     right_hbm,
     counts_hbm,
     neighbours_hbm,
@@ -49,6 +50,7 @@
     windows_coarse,
     sums,
     loads,
+    words,
     *sems,
 ):
     link_sems, relay_sems, pair_sems, far_sems, (sum_send, sum_recv) = [
@@ -73,16 +75,61 @@
         made.start()
     barrier = pltpu.get_barrier_semaphore()
     greeted = 0
+    groups = total // group_size
+    group = me // group_size
     if len(stages) > 1:
         for hop in range(1, HOPS + 1):
             for sign in (1, -1):
                 target = (me + sign * hop + total) % total
                 pl.semaphore_signal(barrier, inc=1, device_id=place(target), device_id_type=MESH)
                 greeted += 1
-    for size, _, peer in stages:
-        for k in range(1, size):
-            pl.semaphore_signal(barrier, inc=1, device_id=peer(k), device_id_type=MESH)
-            greeted += 1
+        for size, _, peer in stages:
+            for k in range(1, size):
+                pl.semaphore_signal(barrier, inc=1, device_id=peer(k), device_id_type=MESH)
+                greeted += 1
+    else:
+        for hop in sorted({*range(1, HOPS + 1), *range(1, group_size + 1)}):
+            for sign in (1, -1):
+                target = me + sign * hop
+                there = (target >= 0) & (target < total)
+                if HOPS < hop < group_size:
+                    there = there & ((target + total) // group_size == group + groups)
+
+                @pl.when(there)
+                def _():
+                    pl.semaphore_signal(
+                        barrier,
+                        inc=1,
+                        device_id=place((target + total) % total),
+                        device_id_type=MESH,
+                    )
+
+                greeted = greeted + there.astype(jnp.int32)
+
+    def pass_word(step):
+        if len(stages) > 1 or step > groups:
+            return
+        sides = ((0, 1, group), (1, -1, groups - 1 - group))
+        if step > 1:
+            for side, _, known in sides:
+
+                @pl.when(known >= step - 1)
+                def _():
+                    pl.semaphore_wait(words.at[side, step - 2], 1)
+
+        if step < groups:
+            for side, sign, known in sides:
+                target = me + sign * group_size
+
+                @pl.when((known >= step - 1) & (target >= 0) & (target < total))
+                def _():
+                    pl.semaphore_signal(
+                        words.at[side, step - 1],
+                        inc=1,
+                        device_id=place((target + total) % total),
+                        device_id_type=MESH,
+                    )
+
     zghost[...] = jnp.zeros_like(zghost)
     yghost_coarse[...] = jnp.zeros_like(yghost_coarse)
     zghost_coarse[...] = jnp.zeros_like(zghost_coarse)
@@ -344,9 +391,11 @@
     cut(first, 8, exchange.faces)
     pl.semaphore_wait(barrier, greeted)
     exchange.post()
+    pass_word(1)
     exchange.near()
     inner(first)
     exchange.forward()
+    pass_word(2)
     exchange.collect()
 
     def sweep(x, rows, outer):
@@ -384,6 +433,7 @@
     inner_rhs = paired[pl.ds(0, 64, 2), :] + paired[pl.ds(1, 64, 2), :]
     smoothed.near()
     sampled.forward()
+    pass_word(3)
     sampled.collect()
     coarse_rhs = 0.125 * (inner_rhs + coarse_outer(sampled.ghosts))
     coarse_one = RELAX_COARSE * coarse_rhs
@@ -406,6 +456,8 @@
     coarse_two = coarse_one + RELAX_COARSE * (coarse_rhs - 0.25 * (6.0 * coarse_one - beside))
     smoothed.forward()
     exchange.forward()
+    for step in range(4, total // group_size + 1):
+        pass_word(step)
     exchange.collect()
     coarse_two = coarse_two + (0.25 * RELAX_COARSE) * coarse_outer(exchange.ghosts)
 
@@ -547,6 +599,7 @@
     cells, lanes = right_side.shape
     curve_size, level_size = sizes
     total = curve_size * level_size
+    group_size = level_size * (2 - curve_size % 2)
 
     def body(*refs):
         curve, level = lax.axis_index("curve"), lax.axis_index("level")
@@ -563,7 +616,7 @@
                 (level_size, level, lambda k: (curve, (level + k) % level_size)),
                 (curve_size, curve, lambda k: ((curve + k) % curve_size, level)),
             ]
-        kernel(sizes, stages, *refs)
+        kernel(sizes, stages, group_size, *refs)
 
     sum_rows = total if total <= 64 else curve_size + level_size
     vmem = pl.BlockSpec(memory_space=pltpu.VMEM)
@@ -595,6 +648,7 @@
             pltpu.VMEM((4, 2, HOPS, 48, lanes), F32),
             pltpu.VMEM((sum_rows, 1, lanes), F32),
             pltpu.SemaphoreType.DMA((3,)),
+            pltpu.SemaphoreType.REGULAR((2, max(1, total // group_size - 1))),
             pltpu.SemaphoreType.DMA((7, 2, 3)),
             pltpu.SemaphoreType.DMA((7, 2, 3)),
             pltpu.SemaphoreType.DMA((7, 2, 3)),

time: 41.6 us -> 40.8 us (0.981)
  Pallas kernels: 40.8 us -> 40 us
    pallas_call x1, Pallas kernels: 39.4 us -> 38.6 us  [local(): pl.pallas_call(body, out_shape=(whole, whole, whole, pltpu.VMEM((1, lanes...]
where the time goes in v4:
time: 40.8 us; the launch traced here: 40.6 us
  Pallas kernels  40 us (98%)
  between operations  0.64 us (2%)
    pallas_call x1, Pallas kernels, local(): pl.pallas_call(body, out_shape=(whole, whole, whole, pltpu.VMEM((1, lanes...  38.6 us
    pallas_call x1, Pallas kernels, local(): pl.pallas_call(finish, out_shape=(block, block, jax.ShapeDtypeStruct((1,)...  1.43 us

profile of v4, /device:TPU:0, one launch (start us, length us, event | category | flops | bytes accessed | tf_op | source)
XLA Modules:
  0.0 40.6 jit_solution(7830883699772529888)
XLA Ops:
  0.6 38.6 %shard_map.58 = (f32[512,128]{1,0:T(8,128)S(1)}, f32[512,128]{1,0:T(8,128)S(1)}, f32[512,128]{1,0:T(8,128)S(1)}, f32[1,128]{1,0:T(1,128)S(1)}) custom-call(f32[512,128]{1,0:T(8,128)} %refs_0_.1, s32[32]{0:T(128)} %refs_1_.1, s32[6,128]{1,0:T(8,128)} %refs_2_.1), custom_call_target="tpu_custom_call" | custom-call | tf_op jit(solution)/shard_map/pallas_call | solution.py:625
  39.2 1.4 %shard_map.59 = (f32[512,128]{1,0:T(8,128)}, f32[512,128]{1,0:T(8,128)}, f32[1]{0:T(128)}) custom-call(f32[512,128]{1,0:T(8,128)S(1)} %get-tuple-element.10.p_ref, f32[512,128]{1,0:T(8,128)S(1)} %get-tuple-element.11.image_ref, f32[512,128]{1,0:T(8,128)S(1)} %get-tuple-element.12.source_ref, f32[1,128]{1,0:T(1,128)S(1)} %get-tuple-element.13.tile_ref), custom_call_target="tpu_custom_call" | custom-call | tf_op jit(solution)/shard_map/pallas_call | solution.py:666

commit v5 on v4

--- a/solution.py
+++ b/solution.py
@@ -166,6 +166,10 @@
         (face_id % 2 == 0) & (hop_of == HOPS), even * (far_count - half), 0
     )
     where_at = jnp.clip(offset - skipped, 0, lanes - 1)
+    skipped = jnp.where((face_id % 2 == 0) & (hop_of == HOPS), far_count - half, 0)
+    where_direct = jnp.clip(offset - skipped, 0, lanes - 1)
+    near_index = jnp.broadcast_to(lane % half, (8, lanes))
+    last_index = near_index + (own_count - half)
     low_half = jnp.broadcast_to(lane < half, (8, lanes))
     pack_index = jnp.broadcast_to(odd * (own_count - half) + lane % half, (8, lanes))
 
@@ -301,18 +305,86 @@
                     pl.when(comes)(relay.wait_recv)
                 self.pull(face, (1, 2, 3))
 
+    class Direct(Exchange):
+        def post(self):
+            faces, packed, windows, stage = self.faces, self.packed, self.windows, self.stage
+            pack = 3 * self.area // 2
+            self.links = []
+
+            def start(hop, direction, src, dst):
+                target = me + hop if direction == 0 else me - hop
+                source_at = me - hop if direction == 0 else me + hop
+                there = (target >= 0) & (target < total)
+                comes = (source_at >= 0) & (source_at < total)
+                at = (stage, direction, hop - 1)
+                made = send(src, dst, link_sems, at, (target + total) % total, there)
+                pl.when(there)(made.start)
+                self.links.append((made, comes))
+
+            for hop in (3, 2, 1):
+                for direction in (0, 1):
+                    if hop < HOPS:
+                        start(hop, direction, faces.at[direction], windows.at[direction, hop - 1])
+                        continue
+                    index = last_index if direction == 0 else near_index
+                    for r in range(0, pack, 8):
+                        a = pick(faces[direction, pl.ds(r, 8), :], index)
+                        b = pick(faces[direction, pl.ds(pack + r, 8), :], index)
+                        packed[direction, pl.ds(r, 8), :] = jnp.where(low_half, a, b)
+                    start(
+                        hop,
+                        direction,
+                        packed.at[direction],
+                        windows.at[direction, hop - 1, pl.ds(0, pack)],
+                    )
+
+        def pull(self, face, hops_in):
+            area, faces, windows = self.area, self.faces, self.windows
+            pack = 3 * area // 2
+            direction, slot = face % 2, face // 2
+            at = jnp.broadcast_to(where_direct[face : face + 1, :], (8, lanes))
+            at_high = jnp.minimum(at + half, lanes - 1)
+            hops = jnp.broadcast_to(hop_of[face : face + 1, :], (8, lanes))
+            for r in range(0, area, 8):
+                row = slot * area + r
+                if 0 in hops_in:
+                    block = jnp.zeros((8, lanes), F32)
+                else:
+                    block = self.ghosts[face, pl.ds(r, 8), :]
+                for hop in hops_in:
+                    if hop == 0:
+                        moved = pick(faces[direction, pl.ds(row, 8), :], at)
+                    elif hop < HOPS:
+                        moved = pick(windows[direction, hop - 1, pl.ds(row, 8), :], at)
+                    else:
+                        window = windows[direction, hop - 1, pl.ds(row % pack, 8), :]
+                        moved = pick(window, at if row < pack else at_high)
+                    block = jnp.where(hops == hop, moved, block)
+                self.ghosts[face, pl.ds(r, 8), :] = block
+
+        def forward(self):
+            pass
+
+        def collect(self):
+            for made, comes in self.links:
+                pl.when(comes)(made.wait_recv)
+            for face in range(6):
+                self.pull(face, (1, 2, 3))
+
     def fine_exchange(k):
         return Exchange(
             k, 64, 3, faces_fine.at[k], packed_fine.at[k], windows_fine.at[k], ghosts_fine.at[k]
         )
 
     def coarse_exchange(k):
-        return Exchange(
+        kind = Direct if k in (1, 3) else Exchange
+        packed = packed_coarse.at[k]
+        return kind(
             3 + k,
             16,
             1,
             faces_coarse.at[k],
-            packed_coarse.at[k],
+            packed if k in (1, 3) else packed.at[0],
             windows_coarse.at[k],
             ghosts_coarse.at[k],
         )
@@ -644,7 +716,7 @@
             pltpu.VMEM((3, 96, lanes), F32),
             pltpu.VMEM((3, 2, HOPS, 192, lanes), F32),
             pltpu.VMEM((4, 2, 48, lanes), F32),
-            pltpu.VMEM((4, 24, lanes), F32),
+            pltpu.VMEM((4, 2, 24, lanes), F32),
             pltpu.VMEM((4, 2, HOPS, 48, lanes), F32),
             pltpu.VMEM((sum_rows, 1, lanes), F32),
             pltpu.SemaphoreType.DMA((3,)),

time: 40.8 us -> 40.2 us (0.985)
  Pallas kernels: 40 us -> 39.4 us
    pallas_call x1, Pallas kernels: 38.6 us -> 38 us  [local(): pl.pallas_call(body, out_shape=(whole, whole, whole, pltpu.VMEM((1, lanes...]
where the time goes in v5:
time: 40.2 us; the launch traced here: 40.1 us
  Pallas kernels  39.4 us (98%)
  between operations  0.64 us (2%)
    pallas_call x1, Pallas kernels, local(): pl.pallas_call(body, out_shape=(whole, whole, whole, pltpu.VMEM((1, lanes...  38 us
    pallas_call x1, Pallas kernels, local(): pl.pallas_call(finish, out_shape=(block, block, jax.ShapeDtypeStruct((1,)...  1.43 us

profile of v5, /device:TPU:0, one launch (start us, length us, event | category | flops | bytes accessed | tf_op | source)
XLA Modules:
  0.0 40.1 jit_solution(194830467095815389)
XLA Ops:
  0.6 38.0 %shard_map.58 = (f32[512,128]{1,0:T(8,128)S(1)}, f32[512,128]{1,0:T(8,128)S(1)}, f32[512,128]{1,0:T(8,128)S(1)}, f32[1,128]{1,0:T(1,128)S(1)}) custom-call(f32[512,128]{1,0:T(8,128)} %refs_0_.1, s32[32]{0:T(128)} %refs_1_.1, s32[6,128]{1,0:T(8,128)} %refs_2_.1), custom_call_target="tpu_custom_call" | custom-call | tf_op jit(solution)/shard_map/pallas_call | solution.py:697
  38.6 1.4 %shard_map.59 = (f32[512,128]{1,0:T(8,128)}, f32[512,128]{1,0:T(8,128)}, f32[1]{0:T(128)}) custom-call(f32[512,128]{1,0:T(8,128)S(1)} %get-tuple-element.10.p_ref, f32[512,128]{1,0:T(8,128)S(1)} %get-tuple-element.11.image_ref, f32[512,128]{1,0:T(8,128)S(1)} %get-tuple-element.12.source_ref, f32[1,128]{1,0:T(1,128)S(1)} %get-tuple-element.13.tile_ref), custom_call_target="tpu_custom_call" | custom-call | tf_op jit(solution)/shard_map/pallas_call | solution.py:738

commit v6 on v5

--- a/solution.py
+++ b/solution.py
@@ -537,7 +537,6 @@
     coarse[0:64, :] = coarse_two
     cut(coarse, 4, corrected.faces)
     corrected.post()
-    corrected.near()
     paired[pl.ds(0, 64, 2), :] = coarse_two
     paired[pl.ds(1, 64, 2), :] = coarse_two
     for x in range(8):
@@ -557,6 +556,7 @@
     almost = fine_exchange(2)
     cut(first, 8, almost.faces)
     almost.post()
+    corrected.near()
     corrected.forward()
     corrected.collect()
 

time: 40.2 us -> 40.2 us (level)
  no operation moved by 1% of the time
where the time goes in v6:
time: 40.2 us; the launch traced here: 40.1 us
  Pallas kernels  39.4 us (98%)
  between operations  0.64 us (2%)
    pallas_call x1, Pallas kernels, local(): pl.pallas_call(body, out_shape=(whole, whole, whole, pltpu.VMEM((1, lanes...  38 us
    pallas_call x1, Pallas kernels, local(): pl.pallas_call(finish, out_shape=(block, block, jax.ShapeDtypeStruct((1,)...  1.43 us

profile of v6, /device:TPU:0, one launch (start us, length us, event | category | flops | bytes accessed | tf_op | source)
XLA Modules:
  0.0 40.1 jit_solution(12336640203595986565)
XLA Ops:
  0.6 38.0 %shard_map.58 = (f32[512,128]{1,0:T(8,128)S(1)}, f32[512,128]{1,0:T(8,128)S(1)}, f32[512,128]{1,0:T(8,128)S(1)}, f32[1,128]{1,0:T(1,128)S(1)}) custom-call(f32[512,128]{1,0:T(8,128)} %refs_0_.1, s32[32]{0:T(128)} %refs_1_.1, s32[6,128]{1,0:T(8,128)} %refs_2_.1), custom_call_target="tpu_custom_call" | custom-call | tf_op jit(solution)/shard_map/pallas_call | solution.py:697
  38.6 1.4 %shard_map.59 = (f32[512,128]{1,0:T(8,128)}, f32[512,128]{1,0:T(8,128)}, f32[1]{0:T(128)}) custom-call(f32[512,128]{1,0:T(8,128)S(1)} %get-tuple-element.10.p_ref, f32[512,128]{1,0:T(8,128)S(1)} %get-tuple-element.11.image_ref, f32[512,128]{1,0:T(8,128)S(1)} %get-tuple-element.12.source_ref, f32[1,128]{1,0:T(1,128)S(1)} %get-tuple-element.13.tile_ref), custom_call_target="tpu_custom_call" | custom-call | tf_op jit(solution)/shard_map/pallas_call | solution.py:738
